TPU v7x, 32 devices: a whole 2x2x4 slice. The times are simulated.
32 devices in a mesh: batch: 4 (over z), seq: 8 (over y, x, core).
Axes of the slice: x: 2, y: 2, z: 4, core: 2. Of those that a mesh axis runs over, the one named last changes fastest.
Arguments:
- tokens: bfloat16 [10240, 8192], P(('batch', 'seq')), may hold values from -6 to 6
- out_grad: bfloat16 [10240, 8192], P(('batch', 'seq')), may hold values from -0.109375 to 0.109375
- gate_pre: bfloat16 [10240, 768], P(('batch', 'seq')), may hold values from -8 to 8
- up_pre: bfloat16 [10240, 768], P(('batch', 'seq')), may hold values from -6 to 6
- hidden_grad: bfloat16 [10240, 768], P(('batch', 'seq')), may hold values from -0.0625 to 0.0625
Outputs:
- gate_weight_grad: float32 [8192, 768], P(('seq', 'batch'))
- up_weight_grad: float32 [8192, 768], P(('seq', 'batch'))
- down_weight_grad: float32 [8192, 768], P(('seq', 'batch'))
All inputs are finite; a program needn't handle non-finite values.
Results may differ from a plain program's by a relative error of at most 0.019.
Values may be sent and summed in bfloat16 or wider, within the bound.
A program may use at most 192 MiB of HBM per device.

v0:
```python
import jax
import jax.numpy as jnp
from jax import lax
from jax.sharding import PartitionSpec as P


def hidden_parts(gate_pre, up_pre, hidden_grad):
    gate_val = gate_pre.astype(jnp.float32)
    up_val = up_pre.astype(jnp.float32)
    grad_val = hidden_grad.astype(jnp.float32)
    sigmoid_val = jax.nn.sigmoid(gate_val)
    activated = gate_val * sigmoid_val
    hidden = (activated * up_val).astype(jnp.bfloat16)
    up_cotangent = (grad_val * activated).astype(jnp.bfloat16)
    gate_cotangent = (
        grad_val * up_val * sigmoid_val * (1.0 + gate_val * (1.0 - sigmoid_val))
    ).astype(jnp.bfloat16)
    return (hidden, gate_cotangent, up_cotangent)


def contract_rows(left, right):
    return lax.dot_general(
        left, right, (((0,), (0,)), ((), ())), preferred_element_type=jnp.float32
    )


def on_device(tokens, out_grad, gate_pre, up_pre, hidden_grad):
    hidden, gate_cotangent, up_cotangent = hidden_parts(gate_pre, up_pre, hidden_grad)
    cotangents = jnp.concatenate([gate_cotangent, up_cotangent], axis=1)
    hidden_width = hidden.shape[1]
    down_total = lax.psum_scatter(
        contract_rows(out_grad, hidden).astype(jnp.bfloat16), "seq", scatter_dimension=0, tiled=True
    ).astype(jnp.float32)
    pair_total = lax.psum_scatter(
        contract_rows(tokens, cotangents).astype(jnp.bfloat16),
        "seq",
        scatter_dimension=0,
        tiled=True,
    ).astype(jnp.float32)
    seq_total = jnp.concatenate([pair_total, down_total], axis=1)
    group_total = lax.psum_scatter(
        seq_total.astype(jnp.bfloat16), "batch", scatter_dimension=0, tiled=True
    ).astype(jnp.float32)
    return (
        group_total[:, :hidden_width],
        group_total[:, hidden_width : 2 * hidden_width],
        group_total[:, 2 * hidden_width :],
    )


def solution(mesh):
    in_specs = (
        P(("batch", "seq"), None),
        P(("batch", "seq"), None),
        P(("batch", "seq"), None),
        P(("batch", "seq"), None),
        P(("batch", "seq"), None),
    )
    out_specs = (P(("seq", "batch"), None), P(("seq", "batch"), None), P(("seq", "batch"), None))
    return jax.shard_map(
        on_device, mesh=mesh, in_specs=in_specs, out_specs=out_specs, check_vma=False
    )
```

profile of v0, /device:TPU:0, one launch (start us, length us, event | category | flops | bytes accessed | tf_op | source)
XLA Modules:
  0.0 375.5 jit_solution(14780036889902649334)
XLA Ops:
  7.2 0.0 reduce-scatter.6.cloned.1.call-start
  7.2 11.8 %fusion.1 = bf16[8192,768]{0,1:T(8,128)(2,1)} fusion(bf16[320,8192]{1,0:T(8,128)(2,1)} %param.6, bf16[320,768]{1,0:T(8,128)(2,1)} %param.8, bf16[320,768]{1,0:T(8,128)(2,1)} %param.7), kind=kOutput, calls=%fused_computation.3 | convolution fusion | flops 4034789376 | bytes 18808832 | tf_op jit(solution)/shard_map/dot_general | solution.py:22
  19.0 0.0 copy-start
  19.0 0.0 copy-start.1
  19.0 0.0 copy-start.2
  19.0 0.0 reduce-scatter.6.cloned.1.call-update
  19.0 0.0 reduce-scatter.4.cloned.1.call-start
  19.1 0.9 copy-done
  20.0 0.1 copy-done.1
  20.2 0.1 copy-done.2
  20.3 0.6 fusion.5
  20.9 20.8 %fusion = bf16[8192,1536]{0,1:T(8,128)(2,1)} fusion(bf16[320,8192]{1,0:T(8,128)(2,1)} %param.5, bf16[320,768]{1,0:T(8,128)(2,1)S(1)} %get-tuple-element.10, bf16[320,768]{1,0:T(8,128)(2,1)S(1)} %get-tuple-element.9), kind=kOutput, calls=%fused_computation.1 | convolution fusion | flops 8067612672 | bytes 31391744 | tf_op jit(solution)/shard_map/dot_general | solution.py:22
  41.7 0.0 reduce-scatter.4.cloned.1.call-update
  41.7 0.0 reduce-scatter.8.cloned.1.call-start
  41.8 72.1 %reduce-scatter.6.cloned.1.call-done = bf16[1024,768]{0,1:T(8,128)(2,1)} async-done(((bf16[8192,768]{0,1:T(8,128)(2,1)}), bf16[1024,768]{0,1:T(8,128)(2,1)}) %reduce-scatter.6.cloned.1.call-update) | async-done | bytes 1572880 | tf_op jit(solution)/shard_map/reduce_scatter | solution.py:31
  113.9 159.7 %reduce-scatter.4.cloned.1.call-done = bf16[1024,1536]{0,1:T(8,128)(2,1)} async-done(((bf16[8192,1536]{0,1:T(8,128)(2,1)}), bf16[1024,1536]{0,1:T(8,128)(2,1)}) %reduce-scatter.4.cloned.1.call-update) | async-done | bytes 3145744 | tf_op jit(solution)/shard_map/reduce_scatter | solution.py:34
  273.6 5.0 %pad_maximum_fusion = bf16[1024,2304]{0,1:T(8,128)(2,1)} fusion(bf16[1024,768]{0,1:T(8,128)(2,1)} %reduce-scatter.6.cloned.1.call-done, bf16[1024,1536]{0,1:T(8,128)(2,1)} %reduce-scatter.4.cloned.1.call-done), kind=kLoop, calls=%fused_computation.4 | loop fusion | flops 9437184 | bytes 9437184 | tf_op jit(solution)/shard_map/concatenate | solution.py:40
  278.6 0.0 reduce-scatter.8.cloned.1.call-update
  278.6 85.5 %reduce-scatter.8.cloned.1.call-done = bf16[256,2304]{0,1:T(8,128)(2,1)} async-done(((bf16[1024,2304]{0,1:T(8,128)(2,1)}), bf16[256,2304]{0,1:T(8,128)(2,1)}) %reduce-scatter.8.cloned.1.call-update) | async-done | bytes 1179664 | tf_op jit(solution)/shard_map/reduce_scatter | solution.py:41
  364.1 1.4 fusion.17
  365.5 1.1 copy.10
  366.7 1.1 copy.8
  367.8 1.1 copy.9
Async XLA Ops:
  7.2 106.7 %reduce-scatter.6.cloned.1.call-start = ((), (), s32[]{:S(2)}) async-start(), calls=%async_computation.4 | async-start | bytes 14155776 | tf_op jit(solution)/shard_map/reduce_scatter | solution.py:31
  19.0 1.0 copy-start
  19.0 1.2 copy-start.1
  19.0 1.3 copy-start.2
  19.0 254.5 %reduce-scatter.4.cloned.1.call-start = ((), (), s32[]{:S(2)}) async-start(), calls=%async_computation.3 | async-start | bytes 28311552 | tf_op jit(solution)/shard_map/reduce_scatter | solution.py:34
  41.7 322.3 %reduce-scatter.8.cloned.1.call-start = ((), (), s32[]{:S(2)}) async-start(), calls=%async_computation.5 | async-start | bytes 5898240 | tf_op jit(solution)/shard_map/reduce_scatter | solution.py:41
Sparse Core Ops, SparseCore 0:
  19.2 94.7 reduce-scatter.5
  117.5 156.0 reduce-scatter.3
  278.7 85.2 reduce-scatter.7
where the time goes:
time: 376 us; the launch traced here: 375 us
  waiting for transfers between devices  317 us (84%)
  matrix products  32.6 us (9%)
  between operations  13.8 us (4%)
  local copies, waits for them, and re-layouts  6.12 us (2%)
  other arithmetic  5.55 us (1%)
    reduce_scatter x1, waiting for transfers between devices, on_device(): lax.psum_scatter(contract_rows(tokens, cotangents).astype(jnp.bfloat16),...  160 us
    reduce_scatter x1, waiting for transfers between devices, on_device(): lax.psum_scatter(seq_total.astype(jnp.bfloat16), 'batch', scatter_dimensi...  85.5 us
    reduce_scatter x1, waiting for transfers between devices, on_device(): lax.psum_scatter(contract_rows(out_grad, hidden).astype(jnp.bfloat16), 's...  72.1 us
    dot_general x2, matrix products, contract_rows(): lax.dot_general(left, right, (((0,), (0,)), ((), ())), preferred_element_...  32.6 us
  transfers between devices with their start and end apart: 3, of which 3 were waited for; matrix products, arithmetic and copies ran while one was open for 6% of the time, Pallas kernels for 0%

commit v1 on v0

v1 whole, which is shorter than its diff:
```python
import functools

import jax
import jax.numpy as jnp
from jax import lax
from jax.experimental import pallas as pl
from jax.experimental.pallas import tpu as pltpu
from jax.sharding import PartitionSpec as P

MESH = pl.DeviceIdType.MESH
LANES = 128


def bit_count(n):
    return n.bit_length() - 1


def flip(value, mask):
    if isinstance(mask, int) and mask == 0:
        return value
    out, bit = 0, 1
    top = mask if isinstance(mask, int) else 1 << 10
    out = value
    while bit <= top:
        if isinstance(mask, int):
            if mask & bit:
                out = out + bit * (1 - 2 * ((value // bit) % 2))
        else:
            out = out + ((mask // bit) % 2) * bit * (1 - 2 * ((value // bit) % 2))
        bit *= 2
    return out


def flip_traced(value, mask, bits):
    out = value
    for i in range(bits):
        bit = 1 << i
        out = out + ((mask // bit) % 2) * bit * (1 - 2 * ((value // bit) % 2))
    return out


class Plan:
    def __init__(self, n_batch, n_seq, tok, width, hidden):
        self.n_batch, self.n_seq, self.tok, self.width, self.hidden = n_batch, n_seq, tok, width, hidden
        self.chips = n_seq // 2
        self.seq_bits, self.batch_bits = bit_count(self.chips), bit_count(n_batch)
        self.rows = width // (n_batch * n_seq)
        self.group = max(1, LANES // self.rows)
        self.block = self.group * self.rows
        self.n_groups = n_batch // self.group
        total = 3 * hidden
        units = total // LANES
        late = max(1, units // 9)
        early = (units - 2 * late) // 2
        cuts = [0, early, units - 2 * late, units - late, units]
        self.spans = [(a * LANES, b * LANES) for a, b in zip(cuts[:-1], cuts[1:])]
        self.ascending = [True, False, True, False]
        self.batch_first = [False, False, True, True]

    def seq_bit(self, cls, stage):
        return stage if self.ascending[cls] else self.seq_bits - 1 - stage

    def position(self, cls, u):
        if not self.ascending[cls]:
            return u
        return sum(((u // (1 << i)) % 2) * (1 << (self.seq_bits - 1 - i)) for i in range(self.seq_bits))

    def pieces(self, lo, hi, step):
        out = []
        while lo < hi:
            end = min(hi, (lo // step + 1) * step)
            out.append((lo, end))
            lo = end
        return out


def low_bit(m):
    return (m & -m).bit_length() - 1


def kernel(plan, tokens, out_grad, gate_pre, up_pre, hidden_grad, out_gate, out_up, out_down, *scratch):
    p = plan
    T, R, M, C, NB = p.tok, p.rows, p.block, p.chips, p.n_batch
    n_cls, sb, bb = len(p.spans), p.seq_bits, p.batch_bits
    scratch = list(scratch)
    raw, hid, tok_v, grad_v = (scratch.pop(0) for _ in range(4))
    terms = [scratch.pop(0) for _ in range(n_cls)]
    seq_in = [[scratch.pop(0) for _ in range(sb)] for _ in range(n_cls)]
    batch_in = [[scratch.pop(0) for _ in range(bb)] for _ in range(n_cls)]
    raw_sem, load_sem, swap_sem, swap_out, seq_send, seq_recv, batch_send, batch_recv = scratch
    outs = (out_gate, out_up, out_down)

    b_me, s_me = lax.axis_index("batch"), lax.axis_index("seq")
    core, chip = s_me % 2, s_me // 2
    twin = (b_me, s_me + 1 - 2 * core)
    seq_peer = [(b_me, flip(s_me, 2 << i)) for i in range(sb)]
    batch_peer = [(flip(b_me, 1 << i), s_me) for i in range(bb)]

    pre = (gate_pre, up_pre, hidden_grad)
    for i, ref in enumerate(pre):
        pltpu.make_async_copy(ref, raw.at[0, i], raw_sem.at[0]).start()

    def column(g, u, side):
        k = flip(chip, u)
        first = flip(b_me // p.group, g) * p.group
        return pl.multiple_of(((k * 2 + side) * NB + first) * R, M)

    sends = []
    groups = list(range(p.n_groups - 1, -1, -1))

    def load(g):
        for a, (src, dst) in enumerate(((tokens, tok_v), (out_grad, grad_v))):
            for u in range(C):
                pltpu.make_async_copy(
                    src.at[:, pl.ds(column(g, u, core), M)], dst.at[g, 0, u], load_sem.at[g, a]
                ).start()

    def swap(g):
        for a, (src, dst) in enumerate(((tokens, tok_v), (out_grad, grad_v))):
            for u in range(C):
                pltpu.make_async_remote_copy(
                    src_ref=src.at[:, pl.ds(column(g, u, 1 - core), M)],
                    dst_ref=dst.at[g, 1, u],
                    send_sem=swap_out.at[g, a],
                    recv_sem=swap_sem.at[g, a],
                    device_id=twin,
                    device_id_type=MESH,
                ).start()

    for g in groups:
        load(g)

    barrier = pltpu.get_barrier_semaphore()
    peers = [twin] + seq_peer + batch_peer
    for peer in peers:
        pl.semaphore_signal(barrier, inc=1, device_id=peer, device_id_type=MESH)
    pl.semaphore_wait(barrier, len(peers))

    for i, ref in enumerate(pre):
        pltpu.make_async_remote_copy(
            src_ref=ref, dst_ref=raw.at[1, i], send_sem=raw_sem.at[1], recv_sem=raw_sem.at[2],
            device_id=twin, device_id_type=MESH,
        ).start()
    for g in groups:
        swap(g)

    def activate(side):
        step = 32
        def body(i, carry):
            at = pl.ds(pl.multiple_of(i * step, step), step)
            gate_val = raw[side, 0, at, :].astype(jnp.float32)
            up_val = raw[side, 1, at, :].astype(jnp.float32)
            grad_val = raw[side, 2, at, :].astype(jnp.float32)
            sig = jax.nn.sigmoid(gate_val)
            act = gate_val * sig
            F = p.hidden
            hid[side, at, 0:F] = (grad_val * up_val * sig * (1.0 + gate_val * (1.0 - sig))).astype(jnp.bfloat16)
            hid[side, at, F:2 * F] = (grad_val * act).astype(jnp.bfloat16)
            hid[side, at, 2 * F:3 * F] = (act * up_val).astype(jnp.bfloat16)
            return carry
        lax.fori_loop(0, T // step, body, 0)

    def wait_bytes(ref, sem):
        pltpu.make_async_copy(ref, ref, sem).wait()

    wait_bytes(raw.at[0], raw_sem.at[0])
    activate(0)
    wait_bytes(raw.at[1], raw_sem.at[2])
    activate(1)

    def dots(lhs, lo, hi):
        total = None
        for side in range(2):
            part = lax.dot_general(
                lhs[side], hid[side, :, lo:hi], (((0,), (0,)), ((), ())), preferred_element_type=jnp.float32
            )
            total = part if total is None else total + part
        return total

    def compute(g):
        for a, dst in enumerate((tok_v, grad_v)):
            wait_bytes(dst.at[g, 0], load_sem.at[g, a])
            wait_bytes(dst.at[g, 1], swap_sem.at[g, a])

        def body(u, carry):
            feats = [tok_v[g, side, u] for side in range(2)]
            grads = [grad_v[g, side, u] for side in range(2)]
            for cls, (lo, hi) in enumerate(p.spans):
                pos = p.position(cls, u)
                for a, b in p.pieces(lo, hi, 2 * p.hidden):
                    value = dots(feats if a < 2 * p.hidden else grads, a, b).astype(jnp.bfloat16)
                    for h in range(p.group):
                        m = g if p.group == 1 else g * p.group + flip(b_me % p.group, h)
                        terms[cls][m, pos, :, a - lo:b - lo] = value[h * R:(h + 1) * R]
            return carry
        lax.fori_loop(0, C, body, 0)

    step = min(R, 32)

    def gather(cls, m, first, count, extra):
        def body(i, carry):
            blk, at = first + i // (R // step), pl.ds(pl.multiple_of((i % (R // step)) * step, step), step)
            value = terms[cls][m, blk, at, :].astype(jnp.float32)
            for ref, slot in extra:
                value = value + ref[slot, blk, at, :].astype(jnp.float32)
            terms[cls][m, blk, at, :] = value.astype(jnp.bfloat16)
            return carry
        if extra:
            lax.fori_loop(0, count * (R // step), body, 0)

    def finish(cls, extra):
        lo, hi = p.spans[cls]
        def body(i, carry):
            at = pl.ds(pl.multiple_of(i * step, step), step)
            for a, b in p.pieces(lo, hi, p.hidden):
                value = terms[cls][0, 0, at, a - lo:b - lo].astype(jnp.float32)
                for ref, slot in extra:
                    value = value + ref[slot, 0, at, a - lo:b - lo].astype(jnp.float32)
                base = (a // p.hidden) * p.hidden
                outs[a // p.hidden][at, a - base:b - base] = value
            return carry
        lax.fori_loop(0, R // step, body, 0)

    def seq_slot(cls, m):
        return 0 if p.batch_first[cls] else m

    def seq_copy(cls, m, stage):
        count = C >> (stage + 1)
        slot = seq_slot(cls, m)
        return pltpu.make_async_remote_copy(
            src_ref=terms[cls].at[m, pl.ds(count, count)],
            dst_ref=seq_in[cls][stage].at[slot],
            send_sem=seq_send.at[cls, stage, slot],
            recv_sem=seq_recv.at[cls, stage, slot],
            device_id=seq_peer[p.seq_bit(cls, stage)],
            device_id_type=MESH,
        )

    def batch_copy(cls, m):
        stage = low_bit(m)
        slot = m >> (stage + 1)
        count = C if p.batch_first[cls] else 1
        return pltpu.make_async_remote_copy(
            src_ref=terms[cls].at[m, pl.ds(0, count)],
            dst_ref=batch_in[cls][stage].at[slot],
            send_sem=batch_send.at[cls, stage, slot],
            recv_sem=batch_recv.at[cls, stage, slot],
            device_id=batch_peer[stage],
            device_id_type=MESH,
        )

    def start(copy):
        copy.start()
        sends.append(copy)

    def from_seq(cls, m, stages):
        return [(seq_in[cls][j], seq_slot(cls, m)) for j in range(stages)]

    def from_batch(cls, m):
        count = bb if m == 0 else low_bit(m)
        return [(batch_in[cls][j], m >> (j + 1)) for j in range(count)]

    def wait_batch(cls, m):
        count = bb if m == 0 else low_bit(m)
        for j in range(count):
            batch_copy(cls, m + (1 << j)).wait_recv()

    def seq_stage(cls, m, stage, base):
        if stage:
            seq_copy(cls, m, stage - 1).wait_recv()
        count = C >> (stage + 1)
        gather(cls, m, count, count, base + from_seq(cls, m, stage))
        start(seq_copy(cls, m, stage))

    def batch_last(cls, m):
        seq_copy(cls, m, sb - 1).wait_recv()
        wait_batch(cls, m)
        extra = from_seq(cls, m, sb) + from_batch(cls, m)
        if m == 0:
            finish(cls, extra)
        else:
            gather(cls, m, 0, 1, extra)
            start(batch_copy(cls, m))

    def batch_early(cls, m):
        wait_batch(cls, m)
        if m:
            gather(cls, m, 0, C, from_batch(cls, m))
            start(batch_copy(cls, m))
        else:
            seq_stage(cls, 0, 0, from_batch(cls, 0))

    plain = [c for c in range(n_cls) if not p.batch_first[c]]
    early = [c for c in range(n_cls) if p.batch_first[c]]
    order = list(range(NB - 1, -1, -1))
    done = set()
    for i in range(NB + 2):
        if i < NB:
            m = order[i]
            if m // p.group not in done:
                done.add(m // p.group)
                compute(m // p.group)
            for cls in plain:
                seq_stage(cls, m, 0, [])
            if m % 2:
                for cls in early:
                    batch_early(cls, m)
        if 1 <= i <= NB:
            m = order[i - 1]
            if m == 0:
                for cls in early:
                    batch_early(cls, m)
            for stage in range(1, sb):
                for cls in plain:
                    seq_stage(cls, m, stage, [])
            if m and m % 2 == 0:
                for cls in early:
                    batch_early(cls, m)
        if i == NB + 1:
            for stage in range(1, sb):
                for cls in early:
                    seq_stage(cls, 0, stage, from_batch(cls, 0))
        if i >= 2:
            for cls in plain:
                batch_last(cls, order[i - 2])
    for cls in early:
        seq_copy(cls, 0, sb - 1).wait_recv()
        finish(cls, from_batch(cls, 0) + from_seq(cls, 0, sb))

    for copy in sends:
        copy.wait_send()
    wait_bytes(raw.at[1], raw_sem.at[1])
    for g in groups:
        for a, dst in enumerate((tok_v, grad_v)):
            wait_bytes(dst.at[g, 1], swap_out.at[g, a])


def on_device(n_batch, n_seq, tokens, out_grad, gate_pre, up_pre, hidden_grad):
    tok, width = tokens.shape
    hidden = gate_pre.shape[1]
    p = Plan(n_batch, n_seq, tok, width, hidden)
    C, R, bf16 = p.chips, p.rows, jnp.bfloat16
    scratch = [
        pltpu.VMEM((2, 3, tok, hidden), bf16),
        pltpu.VMEM((2, tok, 3 * hidden), bf16),
        pltpu.VMEM((p.n_groups, 2, C, tok, p.block), bf16),
        pltpu.VMEM((p.n_groups, 2, C, tok, p.block), bf16),
    ]
    sizes = [hi - lo for lo, hi in p.spans]
    scratch += [pltpu.VMEM((n_batch, C, R, size), bf16) for size in sizes]
    for cls, size in enumerate(sizes):
        slots = 1 if p.batch_first[cls] else n_batch
        scratch += [pltpu.VMEM((slots, C >> (j + 1), R, size), bf16) for j in range(p.seq_bits)]
    for cls, size in enumerate(sizes):
        blocks = C if p.batch_first[cls] else 1
        scratch += [pltpu.VMEM((n_batch >> (j + 1), blocks, R, size), bf16) for j in range(p.batch_bits)]
    n_cls = len(sizes)
    dma = pltpu.SemaphoreType.DMA
    scratch += [
        dma((3,)),
        dma((p.n_groups, 2)), dma((p.n_groups, 2)), dma((p.n_groups, 2)),
        dma((n_cls, p.seq_bits, n_batch)), dma((n_cls, p.seq_bits, n_batch)),
        dma((n_cls, p.batch_bits, n_batch // 2)), dma((n_cls, p.batch_bits, n_batch // 2)),
    ]
    out = jax.ShapeDtypeStruct((R, hidden), jnp.float32)
    return pl.pallas_call(
        functools.partial(kernel, p),
        out_shape=(out, out, out),
        in_specs=[pl.BlockSpec(memory_space=pltpu.HBM)] * 5,
        out_specs=[pl.BlockSpec(memory_space=pltpu.VMEM)] * 3,
        scratch_shapes=scratch,
        compiler_params=pltpu.CompilerParams(
            collective_id=0, has_side_effects=True, vmem_limit_bytes=67043328
        ),
    )(tokens, out_grad, gate_pre, up_pre, hidden_grad)


def solution(mesh):
    rows = P(("batch", "seq"), None)
    outs = P(("seq", "batch"), None)
    body = functools.partial(on_device, mesh.shape["batch"], mesh.shape["seq"])
    return jax.shard_map(
        body, mesh=mesh, in_specs=(rows,) * 5, out_specs=(outs,) * 3, check_vma=False
    )
```

time: 376 us -> 172 us (0.46)
  waiting for transfers between devices: 317 us -> 0 us
  Pallas kernels: 0 us -> 165 us
  matrix products: 32.6 us -> 0 us
  between operations: 13.8 us -> 0.64 us
  other arithmetic: 5.55 us -> 0 us
    reduce_scatter x3 -> x0, waiting for transfers between devices: 317 us -> none  [the longest x1 160 us: on_device(): lax.psum_scatter(contract_rows(tokens, cotangents).astype(jnp.bfloat16),...]
    pallas_call x0 -> x1, Pallas kernels: none -> 165 us  [on_device(): pl.pallas_call(functools.partial(kernel, p), out_shape=(out, out, out), i...]
    dot_general x2 -> x0, matrix products: 32.6 us -> none  [contract_rows(): lax.dot_general(left, right, (((0,), (0,)), ((), ())), preferred_element_...]
    concatenate x1 -> x0, other arithmetic: 5 us -> none  [on_device(): seq_total = jnp.concatenate([pair_total, down_total], axis=1)]
  transfers between devices with their start and end apart: 3 -> 0, of which waited for: 3 -> 0; matrix products, arithmetic and copies ran while one was open for 6% -> 0% of each run, Pallas kernels for 0% -> 0%
where the time goes in v1:
time: 172 us
  Pallas kernels  165 us (96%)
  local copies, waits for them, and re-layouts  6.19 us (4%)
    pallas_call x1, Pallas kernels, on_device(): pl.pallas_call(functools.partial(kernel, p), out_shape=(out, out, out), i...  165 us
    unnamed x3, local copies, waits for them, and re-layouts  6.19 us

profile of v1, /device:TPU:0, one launch (start us, length us, event | category | flops | bytes accessed | tf_op | source)
XLA Modules:
  0.0 171.6 jit_solution(3347346900773897103)
XLA Ops:
  0.6 164.8 %shard_map.76 = (f32[256,768]{1,0:T(8,128)}, f32[256,768]{1,0:T(8,128)}, f32[256,768]{1,0:T(8,128)}) custom-call(bf16[320,8192]{1,0:T(8,128)(2,1)} %tokens.1, bf16[320,8192]{1,0:T(8,128)(2,1)} %out_grad.1, bf16[320,768]{1,0:T(8,128)(2,1)} %gate_pre.1, bf16[320,768]{1,0:T(8,128)(2,1)} %up_pre.1, bf16[320,768]{1,0:T(8,128)(2,1)} %hidden_grad.1), custom_call_target="tpu_custom_call" | custom-call | tf_op jit(solution)/shard_map/pallas_call | solution.py:366
  165.4 2.1 %copy.11 = f32[256,768]{1,0:T(8,128)} copy(f32[256,768]{1,0:T(8,128)} %get-tuple-element.6) | data formatting | bytes 1572864
  167.5 2.1 %copy.12 = f32[256,768]{1,0:T(8,128)} copy(f32[256,768]{1,0:T(8,128)} %get-tuple-element.7) | data formatting | bytes 1572864
  169.6 2.1 %copy.13 = f32[256,768]{1,0:T(8,128)} copy(f32[256,768]{1,0:T(8,128)} %get-tuple-element.8) | data formatting | bytes 1572864

commit v2 on v1

--- a/solution.py
+++ b/solution.py
@@ -16,26 +16,11 @@
 
 
 def flip(value, mask):
-    if isinstance(mask, int) and mask == 0:
-        return value
-    out, bit = 0, 1
-    top = mask if isinstance(mask, int) else 1 << 10
-    out = value
-    while bit <= top:
-        if isinstance(mask, int):
-            if mask & bit:
-                out = out + bit * (1 - 2 * ((value // bit) % 2))
-        else:
-            out = out + ((mask // bit) % 2) * bit * (1 - 2 * ((value // bit) % 2))
+    out, bit = value, 1
+    while bit <= mask:
+        if mask & bit:
+            out = out + bit * (1 - 2 * ((value // bit) % 2))
         bit *= 2
-    return out
-
-
-def flip_traced(value, mask, bits):
-    out = value
-    for i in range(bits):
-        bit = 1 << i
-        out = out + ((mask // bit) % 2) * bit * (1 - 2 * ((value // bit) % 2))
     return out
 
 
@@ -98,7 +83,7 @@
 
     pre = (gate_pre, up_pre, hidden_grad)
     for i, ref in enumerate(pre):
-        pltpu.make_async_copy(ref, raw.at[0, i], raw_sem.at[0]).start()
+        pltpu.make_async_copy(ref, raw.at[i, pl.ds(0, T)], raw_sem.at[0]).start()
 
     def column(g, u, side):
         k = flip(chip, u)
@@ -112,7 +97,7 @@
         for a, (src, dst) in enumerate(((tokens, tok_v), (out_grad, grad_v))):
             for u in range(C):
                 pltpu.make_async_copy(
-                    src.at[:, pl.ds(column(g, u, core), M)], dst.at[g, 0, u], load_sem.at[g, a]
+                    src.at[:, pl.ds(column(g, u, core), M)], dst.at[g, u, pl.ds(0, T)], load_sem.at[g, a]
                 ).start()
 
     def swap(g):
@@ -120,7 +105,7 @@
             for u in range(C):
                 pltpu.make_async_remote_copy(
                     src_ref=src.at[:, pl.ds(column(g, u, 1 - core), M)],
-                    dst_ref=dst.at[g, 1, u],
+                    dst_ref=dst.at[g, u, pl.ds(T, T)],
                     send_sem=swap_out.at[g, a],
                     recv_sem=swap_sem.at[g, a],
                     device_id=twin,
@@ -138,7 +123,7 @@
 
     for i, ref in enumerate(pre):
         pltpu.make_async_remote_copy(
-            src_ref=ref, dst_ref=raw.at[1, i], send_sem=raw_sem.at[1], recv_sem=raw_sem.at[2],
+            src_ref=ref, dst_ref=raw.at[i, pl.ds(T, T)], send_sem=raw_sem.at[1], recv_sem=raw_sem.at[2],
             device_id=twin, device_id_type=MESH,
         ).start()
     for g in groups:
@@ -147,51 +132,50 @@
     def activate(side):
         step = 32
         def body(i, carry):
-            at = pl.ds(pl.multiple_of(i * step, step), step)
-            gate_val = raw[side, 0, at, :].astype(jnp.float32)
-            up_val = raw[side, 1, at, :].astype(jnp.float32)
-            grad_val = raw[side, 2, at, :].astype(jnp.float32)
+            at = pl.ds(pl.multiple_of(side * T + i * step, step), step)
+            gate_val = raw[0, at, :].astype(jnp.float32)
+            up_val = raw[1, at, :].astype(jnp.float32)
+            grad_val = raw[2, at, :].astype(jnp.float32)
             sig = jax.nn.sigmoid(gate_val)
             act = gate_val * sig
             F = p.hidden
-            hid[side, at, 0:F] = (grad_val * up_val * sig * (1.0 + gate_val * (1.0 - sig))).astype(jnp.bfloat16)
-            hid[side, at, F:2 * F] = (grad_val * act).astype(jnp.bfloat16)
-            hid[side, at, 2 * F:3 * F] = (act * up_val).astype(jnp.bfloat16)
+            hid[at, 0:F] = (grad_val * up_val * sig * (1.0 + gate_val * (1.0 - sig))).astype(jnp.bfloat16)
+            hid[at, F:2 * F] = (grad_val * act).astype(jnp.bfloat16)
+            hid[at, 2 * F:3 * F] = (act * up_val).astype(jnp.bfloat16)
             return carry
         lax.fori_loop(0, T // step, body, 0)
 
     def wait_bytes(ref, sem):
         pltpu.make_async_copy(ref, ref, sem).wait()
 
-    wait_bytes(raw.at[0], raw_sem.at[0])
+    wait_bytes(raw.at[:, pl.ds(0, T)], raw_sem.at[0])
     activate(0)
-    wait_bytes(raw.at[1], raw_sem.at[2])
+    wait_bytes(raw.at[:, pl.ds(T, T)], raw_sem.at[2])
     activate(1)
 
-    def dots(lhs, lo, hi):
-        total = None
-        for side in range(2):
-            part = lax.dot_general(
-                lhs[side], hid[side, :, lo:hi], (((0,), (0,)), ((), ())), preferred_element_type=jnp.float32
-            )
-            total = part if total is None else total + part
-        return total
+    def arrive(g):
+        for a, dst in enumerate((tok_v, grad_v)):
+            wait_bytes(dst.at[g, :, pl.ds(0, T)], load_sem.at[g, a])
+            wait_bytes(dst.at[g, :, pl.ds(T, T)], swap_sem.at[g, a])
+
+    def compute_block(g, u):
+        feats, grads = tok_v[g, u], grad_v[g, u]
+        for cls, (lo, hi) in enumerate(p.spans):
+            pos = p.position(cls, u)
+            for a, b in p.pieces(lo, hi, 2 * p.hidden):
+                value = lax.dot_general(
+                    feats if a < 2 * p.hidden else grads, hid[:, a:b],
+                    (((0,), (0,)), ((), ())), preferred_element_type=jnp.float32,
+                ).astype(jnp.bfloat16)
+                for h in range(p.group):
+                    m = g if p.group == 1 else g * p.group + flip(b_me % p.group, h)
+                    terms[cls][m, pos, :, a - lo:b - lo] = value[h * R:(h + 1) * R]
 
     def compute(g):
-        for a, dst in enumerate((tok_v, grad_v)):
-            wait_bytes(dst.at[g, 0], load_sem.at[g, a])
-            wait_bytes(dst.at[g, 1], swap_sem.at[g, a])
+        arrive(g)
 
         def body(u, carry):
-            feats = [tok_v[g, side, u] for side in range(2)]
-            grads = [grad_v[g, side, u] for side in range(2)]
-            for cls, (lo, hi) in enumerate(p.spans):
-                pos = p.position(cls, u)
-                for a, b in p.pieces(lo, hi, 2 * p.hidden):
-                    value = dots(feats if a < 2 * p.hidden else grads, a, b).astype(jnp.bfloat16)
-                    for h in range(p.group):
-                        m = g if p.group == 1 else g * p.group + flip(b_me % p.group, h)
-                        terms[cls][m, pos, :, a - lo:b - lo] = value[h * R:(h + 1) * R]
+            compute_block(g, u)
             return carry
         lax.fori_loop(0, C, body, 0)
 
@@ -224,14 +208,19 @@
     def seq_slot(cls, m):
         return 0 if p.batch_first[cls] else m
 
-    def seq_copy(cls, m, stage):
+    def halves(stage):
+        return 2 if C >> (stage + 1) > 1 else 1
+
+    def seq_copy(cls, m, stage, part):
         count = C >> (stage + 1)
+        size = count // halves(stage)
+        first = count - size if part == 0 else 0
         slot = seq_slot(cls, m)
         return pltpu.make_async_remote_copy(
-            src_ref=terms[cls].at[m, pl.ds(count, count)],
-            dst_ref=seq_in[cls][stage].at[slot],
-            send_sem=seq_send.at[cls, stage, slot],
-            recv_sem=seq_recv.at[cls, stage, slot],
+            src_ref=terms[cls].at[m, pl.ds(count + first, size)],
+            dst_ref=seq_in[cls][stage].at[slot, pl.ds(first, size)],
+            send_sem=seq_send.at[cls, 2 * stage + part, slot],
+            recv_sem=seq_recv.at[cls, 2 * stage + part, slot],
             device_id=seq_peer[p.seq_bit(cls, stage)],
             device_id_type=MESH,
         )
@@ -265,15 +254,21 @@
         for j in range(count):
             batch_copy(cls, m + (1 << j)).wait_recv()
 
-    def seq_stage(cls, m, stage, base):
-        if stage:
-            seq_copy(cls, m, stage - 1).wait_recv()
+    def wait_seq(cls, m, stage):
+        if stage >= 0:
+            seq_copy(cls, m, stage, 0).wait_recv()
+        if stage >= 1:
+            seq_copy(cls, m, stage - 1, 1).wait_recv()
+
+    def seq_stage(cls, m, stage, base, parts=(0, 1)):
+        wait_seq(cls, m, stage - 1)
         count = C >> (stage + 1)
         gather(cls, m, count, count, base + from_seq(cls, m, stage))
-        start(seq_copy(cls, m, stage))
+        for part in parts[:halves(stage)]:
+            start(seq_copy(cls, m, stage, part))
 
     def batch_last(cls, m):
-        seq_copy(cls, m, sb - 1).wait_recv()
+        wait_seq(cls, m, sb - 1)
         wait_batch(cls, m)
         extra = from_seq(cls, m, sb) + from_batch(cls, m)
         if m == 0:
@@ -294,45 +289,74 @@
     early = [c for c in range(n_cls) if p.batch_first[c]]
     order = list(range(NB - 1, -1, -1))
     done = set()
-    for i in range(NB + 2):
+
+    def need(i):
+        if i < NB and order[i] // p.group not in done:
+            done.add(order[i] // p.group)
+            compute(order[i] // p.group)
+
+    def first_round():
+        g = groups[0]
+        done.add(g)
+        arrive(g)
+        upper = [u for u in range(C) if any(p.position(c, u) >= C - C // 4 for c in plain)] if p.group == 1 else []
+        for u in upper:
+            compute_block(g, u)
+        split = bool(upper) and halves(0) == 2
+        if split:
+            for cls in plain:
+                start(seq_copy(cls, order[0], 0, 0))
+        rest = [u for u in range(C) if u not in upper]
+        if rest == list(range(len(rest))):
+            def body(u, carry):
+                compute_block(g, u)
+                return carry
+            lax.fori_loop(0, len(rest), body, 0)
+        else:
+            for u in rest:
+                compute_block(g, u)
+        for cls in plain:
+            for part in range(1 if split else 0, halves(0)):
+                start(seq_copy(cls, order[0], 0, part))
+        if order[0] % 2:
+            for cls in early:
+                batch_early(cls, order[0])
+
+    first_round()
+    for i in range(1, NB + 1):
+        before = order[i - 1]
+        need(i)
+        if i == 1:
+            need(2)
+        for stage in range(1, sb):
+            for cls in plain:
+                seq_stage(cls, before, stage, [])
         if i < NB:
-            m = order[i]
-            if m // p.group not in done:
-                done.add(m // p.group)
-                compute(m // p.group)
             for cls in plain:
-                seq_stage(cls, m, 0, [])
-            if m % 2:
-                for cls in early:
-                    batch_early(cls, m)
-        if 1 <= i <= NB:
-            m = order[i - 1]
-            if m == 0:
-                for cls in early:
-                    batch_early(cls, m)
-            for stage in range(1, sb):
-                for cls in plain:
-                    seq_stage(cls, m, stage, [])
-            if m and m % 2 == 0:
-                for cls in early:
-                    batch_early(cls, m)
-        if i == NB + 1:
+                seq_stage(cls, order[i], 0, [])
+        if i + 1 < NB:
+            need(i + 1)
+        for cls in early:
+            if i + 1 < NB and order[i + 1] % 2:
+                batch_early(cls, order[i + 1])
+            if i < NB and order[i] % 2 == 0:
+                batch_early(cls, order[i])
+        if i == NB:
             for stage in range(1, sb):
                 for cls in early:
                     seq_stage(cls, 0, stage, from_batch(cls, 0))
-        if i >= 2:
-            for cls in plain:
-                batch_last(cls, order[i - 2])
+        for cls in plain:
+            batch_last(cls, before)
     for cls in early:
-        seq_copy(cls, 0, sb - 1).wait_recv()
+        wait_seq(cls, 0, sb - 1)
         finish(cls, from_batch(cls, 0) + from_seq(cls, 0, sb))
 
     for copy in sends:
         copy.wait_send()
-    wait_bytes(raw.at[1], raw_sem.at[1])
+    wait_bytes(raw.at[:, pl.ds(T, T)], raw_sem.at[1])
     for g in groups:
         for a, dst in enumerate((tok_v, grad_v)):
-            wait_bytes(dst.at[g, 1], swap_out.at[g, a])
+            wait_bytes(dst.at[g, :, pl.ds(T, T)], swap_out.at[g, a])
 
 
 def on_device(n_batch, n_seq, tokens, out_grad, gate_pre, up_pre, hidden_grad):
@@ -341,10 +365,10 @@
     p = Plan(n_batch, n_seq, tok, width, hidden)
     C, R, bf16 = p.chips, p.rows, jnp.bfloat16
     scratch = [
-        pltpu.VMEM((2, 3, tok, hidden), bf16),
-        pltpu.VMEM((2, tok, 3 * hidden), bf16),
-        pltpu.VMEM((p.n_groups, 2, C, tok, p.block), bf16),
-        pltpu.VMEM((p.n_groups, 2, C, tok, p.block), bf16),
+        pltpu.VMEM((3, 2 * tok, hidden), bf16),
+        pltpu.VMEM((2 * tok, 3 * hidden), bf16),
+        pltpu.VMEM((p.n_groups, C, 2 * tok, p.block), bf16),
+        pltpu.VMEM((p.n_groups, C, 2 * tok, p.block), bf16),
     ]
     sizes = [hi - lo for lo, hi in p.spans]
     scratch += [pltpu.VMEM((n_batch, C, R, size), bf16) for size in sizes]
@@ -359,7 +383,7 @@
     scratch += [
         dma((3,)),
         dma((p.n_groups, 2)), dma((p.n_groups, 2)), dma((p.n_groups, 2)),
-        dma((n_cls, p.seq_bits, n_batch)), dma((n_cls, p.seq_bits, n_batch)),
+        dma((n_cls, 2 * p.seq_bits, n_batch)), dma((n_cls, 2 * p.seq_bits, n_batch)),
         dma((n_cls, p.batch_bits, n_batch // 2)), dma((n_cls, p.batch_bits, n_batch // 2)),
     ]
     out = jax.ShapeDtypeStruct((R, hidden), jnp.float32)

time: 172 us -> 173 us (level)
  no operation moved by 1% of the time
where the time goes in v2:
time: 173 us; the launch traced here: 172 us
  Pallas kernels  166 us (96%)
  local copies, waits for them, and re-layouts  6.19 us (4%)
    pallas_call x1, Pallas kernels, on_device(): pl.pallas_call(functools.partial(kernel, p), out_shape=(out, out, out), i...  166 us
    unnamed x3, local copies, waits for them, and re-layouts  6.19 us

profile of v2, /device:TPU:0, one launch (start us, length us, event | category | flops | bytes accessed | tf_op | source)
XLA Modules:
  0.0 172.4 jit_solution(2495031138269218903)
XLA Ops:
  0.6 165.6 %shard_map.76 = (f32[256,768]{1,0:T(8,128)}, f32[256,768]{1,0:T(8,128)}, f32[256,768]{1,0:T(8,128)}) custom-call(bf16[320,8192]{1,0:T(8,128)(2,1)} %tokens.1, bf16[320,8192]{1,0:T(8,128)(2,1)} %out_grad.1, bf16[320,768]{1,0:T(8,128)(2,1)} %gate_pre.1, bf16[320,768]{1,0:T(8,128)(2,1)} %up_pre.1, bf16[320,768]{1,0:T(8,128)(2,1)} %hidden_grad.1), custom_call_target="tpu_custom_call" | custom-call | tf_op jit(solution)/shard_map/pallas_call | solution.py:390
  166.3 2.1 %copy.11 = f32[256,768]{1,0:T(8,128)} copy(f32[256,768]{1,0:T(8,128)} %get-tuple-element.6) | data formatting | bytes 1572864
  168.3 2.1 %copy.12 = f32[256,768]{1,0:T(8,128)} copy(f32[256,768]{1,0:T(8,128)} %get-tuple-element.7) | data formatting | bytes 1572864
  170.4 2.1 %copy.13 = f32[256,768]{1,0:T(8,128)} copy(f32[256,768]{1,0:T(8,128)} %get-tuple-element.8) | data formatting | bytes 1572864
